TPU v7x, 32 devices: a whole 2x2x4 slice. The times are simulated.
32 devices in a mesh: grid: 8 (over y, x, core), band: 4 (over z).
Axes of the slice: x: 2, y: 2, z: 4, core: 2. Of those that a mesh axis runs over, the one named last changes fastest.
Arguments:
- start: float32 [1, 4, 1, 64, 32768], P(None, None, None, 'band', 'grid'), may hold values from -6 to 6
- energies: float32 [4, 64, 32768], P(None, 'band', 'grid'), may hold values from -4 to 4
- sites: int32 [3, 1], replicated, may hold values from 0 to 31
- potential: float32 [32, 32, 32], replicated, may hold values from -4 to 400
Outputs:
- alphas: float32 [1, 1, 4], replicated
- betas: float32 [1, 1, 4], replicated
- lanczos: float32 [1, 4, 1, 64, 32768], P(None, None, None, 'band', 'grid')
All inputs are finite; a program needn't handle non-finite values.
Results may differ from a plain program's by a relative error of at most 0.0003.
Values sent between devices are 32-bit elements; how exact they have to be, the bound alone decides.
A program may use at most 64 MiB of HBM per device.

v0:
```python
import math
import jax
import jax.numpy as jnp
from jax import lax
from jax.sharding import PartitionSpec as P

ITERS = 4
precise_mode = lax.Precision.HIGHEST


def cas_table(grid_size):
    cells = jnp.arange(grid_size, dtype=jnp.int32)
    phase = cells[:, None] * cells[None, :] % grid_size
    angle = phase.astype(jnp.float32) * (2.0 * math.pi / grid_size)
    return jnp.cos(angle) + jnp.sin(angle)


def shift_axis(field_part, offset, axis_number):
    length = field_part.shape[axis_number]
    doubled = jnp.concatenate([field_part, field_part], axis=axis_number)
    first_index = (length - offset) % length
    return lax.dynamic_slice_in_dim(doubled, first_index, length, axis_number)


def expand_coef(values):
    return values[:, None, :, None, None]


def body(start, energies, sites, potential):
    grid_size = potential.shape[0]
    volume = grid_size * grid_size * grid_size
    atom_count, core_count, pol_count, band_local, kpoint_local = start.shape
    plane_count = grid_size // lax.axis_size("grid")
    position = lax.axis_index("grid")
    chain_count = core_count * pol_count * band_local
    field_count = atom_count * chain_count
    total_count = (
        core_count * band_local * lax.axis_size("band") * kpoint_local * lax.axis_size("grid")
    )
    cas_grid = cas_table(grid_size)
    shifted = shift_axis(potential, sites[0, 0], 0)
    shifted = shift_axis(shifted, sites[1, 0], 1)
    shifted = shift_axis(shifted, sites[2, 0], 2)
    tables = [shifted]
    shifted_all = jnp.stack(tables, axis=-1)
    slab_table = lax.dynamic_slice_in_dim(shifted_all, position * plane_count, plane_count, 1)

    def moment(left, right):
        return jnp.sum(left * right, axis=(1, 3, 4)) / total_count

    start_sum = lax.psum(moment(start, start), ("grid", "band"))
    lanczos = start / expand_coef(jnp.sqrt(start_sum))
    previous = jnp.zeros_like(start)
    beta_prev = jnp.zeros((atom_count, pol_count), jnp.float32)
    alpha_list = []
    beta_list = []
    for iteration in range(ITERS):
        spread_fields = lanczos.reshape(atom_count, chain_count, plane_count, grid_size, grid_size)
        spread_over_z = jnp.einsum(
            "arpyz,wz->pywar", spread_fields, cas_grid, precision=precise_mode
        )
        spread_over_y = jnp.einsum(
            "pywar,uy->puwar", spread_over_z, cas_grid, precision=precise_mode
        )
        direct_spectrum = lax.all_to_all(
            spread_over_y.reshape(plane_count, grid_size, grid_size, field_count),
            "grid",
            split_axis=1,
            concat_axis=0,
            tiled=True,
        )
        field_shape = direct_spectrum.shape
        over_x = jnp.einsum("xvwf,tx->tvwf", direct_spectrum, cas_grid, precision=precise_mode)
        split_view = over_x.reshape(
            field_shape[0], field_shape[1], field_shape[2], atom_count, chain_count
        )
        scaled = split_view * slab_table[..., None]
        back_x = jnp.einsum("tvwar,xt->xvwar", scaled, cas_grid, precision=precise_mode)
        weighted = back_x.reshape(field_shape)
        direct_returned = lax.all_to_all(weighted, "grid", split_axis=0, concat_axis=1, tiled=True)
        fields = direct_returned.reshape(plane_count, grid_size, grid_size, atom_count, chain_count)
        over_z = jnp.einsum("pvwar,zw->pvzar", fields, cas_grid, precision=precise_mode)
        over_y = jnp.einsum("pvzar,yv->arpyz", over_z, cas_grid, precision=precise_mode)
        applied = energies[None, :, None] * lanczos - over_y.reshape(start.shape) / volume
        moments_all = lax.psum(
            (
                moment(lanczos, applied),
                moment(applied, applied),
                moment(lanczos, lanczos),
                moment(previous, previous),
                moment(previous, applied),
                moment(lanczos, previous),
            ),
            ("grid", "band"),
        )
        alpha_now = moments_all[0]
        square = (
            moments_all[1]
            + alpha_now * alpha_now * moments_all[2]
            + beta_prev * beta_prev * moments_all[3]
        )
        square = square - 2.0 * alpha_now * moments_all[0] - 2.0 * beta_prev * moments_all[4]
        square = square + 2.0 * alpha_now * beta_prev * moments_all[5]
        beta_now = jnp.sqrt(square)
        remainder = applied - expand_coef(alpha_now) * lanczos - expand_coef(beta_prev) * previous
        previous = lanczos
        lanczos = remainder / expand_coef(beta_now)
        beta_prev = beta_now
        alpha_list.append(alpha_now)
        beta_list.append(beta_now)
    return (jnp.stack(alpha_list, axis=2), jnp.stack(beta_list, axis=2), lanczos)


def solution(mesh):
    in_specs = (P(None, None, None, "band", "grid"), P(None, "band", "grid"), P(), P())
    out_specs = (P(), P(), P(None, None, None, "band", "grid"))
    return jax.shard_map(body, mesh=mesh, in_specs=in_specs, out_specs=out_specs, check_vma=False)
```

profile of v0, /device:TPU:0, one launch (start us, length us, event | category | flops | bytes accessed | tf_op | source)
XLA Modules:
  0.0 697.9 jit_solution(12863842465715470932)
XLA Ops:
  3.4 42.7 %psum.163 = f32[1,1]{1,0:T(1,128)} all-reduce(f32[1,1]{1,0:T(1,128)} %bitcast.1), channel_id=1, replica_groups=mesh['grid'=8,'band'=4] {'grid','band'}, use_global_device_ids=true, to_apply=%region_1.2 | all-reduce | flops 1 | bytes 8 | tf_op jit(solution)/shard_map/psum | solution.py:51
  50.7 14.6 %fusion.60 = f32[4,32,32,64]{3,2,1,0:T(8,128)S(1)} fusion(f32[64,4,32,32]{3,2,1,0:T(8,128)} %reshape.300), kind=kOutput, calls=%fused_computation.48 | convolution fusion | flops 100678656 | bytes 2097152 | tf_op jit(solution)/shard_map/arpyz,wz->pywar/dot_general | solution.py:59
  79.0 12.1 %all-to-all-done = f32[8,1,32768]{2,1,0:T(1,128)S(1)} async-done(((f32[8,1,32768]{2,1,0:T(1,128)}), f32[8,1,32768]{2,1,0:T(1,128)S(1)}, u32[]{:S(2)}, u32[]{:S(2)}) %all-to-all-start) | async-done | bytes 1048608 | tf_op jit(solution)/shard_map/all_to_all | solution.py:65
  103.6 18.2 %all_to_all.132 = f32[8,1,32768]{2,1,0:T(1,128)S(1)} all-to-all(f32[8,1,32768]{2,1,0:T(1,128)S(1)} %reshape.323), channel_id=1, replica_groups=mesh['grid'=8,'band'=4] {'grid'}, dimensions={0} | all-to-all | bytes 2097152 | tf_op jit(solution)/shard_map/all_to_all | solution.py:80
  130.9 4.5 copy.97
  144.4 43.1 %all-reduce.3 = (f32[1,1]{1,0:T(1,128)}, f32[1,1]{1,0:T(1,128)}, f32[1,1]{1,0:T(1,128)}, f32[1,1]{1,0:T(1,128)}, f32[1,1]{1,0:T(1,128)}, /*index=5*/f32[1,1]{1,0:T(1,128)}) all-reduce(f32[1,1]{1,0:T(1,128)} %bitcast.31, f32[1,1]{1,0:T(1,128)} %bitcast.28, f32[1,1]{1,0:T(1,128)} %bitcast.32, ...), channel_id=1, replica_groups=mesh['grid'=8,'band'=4] {'grid','band'}, use_global_device_ids=true, to_apply=%region_5.6 | all-reduce | flops 6 | bytes 48 | tf_op jit(solution)/shard_map/psum | solution.py:85
  198.1 14.6 %fusion.63 = f32[4,32,32,64]{3,2,1,0:T(8,128)S(1)} fusion(f32[64,4,32,32]{3,2,1,0:T(8,128)} %reshape.305), kind=kOutput, calls=%fused_computation.49 | convolution fusion | flops 100678656 | bytes 2097152 | tf_op jit(solution)/shard_map/arpyz,wz->pywar/dot_general | solution.py:59
  221.6 19.8 %all_to_all.133 = f32[8,1,32768]{2,1,0:T(1,128)} all-to-all(f32[8,1,32768]{2,1,0:T(1,128)} %reshape.325), channel_id=1, replica_groups=mesh['grid'=8,'band'=4] {'grid'}, dimensions={0} | all-to-all | bytes 2097152 | tf_op jit(solution)/shard_map/all_to_all | solution.py:65
  241.4 5.3 reduce.23
  263.0 4.6 all-to-all-start.3
  268.3 14.8 %all-to-all-done.3 = f32[8,1,32768]{2,1,0:T(1,128)} async-done(((f32[8,1,32768]{2,1,0:T(1,128)}), f32[8,1,32768]{2,1,0:T(1,128)}, u32[]{:S(2)}, u32[]{:S(2)}) %all-to-all-start.3) | async-done | bytes 1048608 | tf_op jit(solution)/shard_map/all_to_all | solution.py:80
  283.1 5.3 reduce.24
  295.6 4.4 multiply_bitcast_fusion.2
  299.9 5.6 copy.107
  316.3 41.5 %all-reduce.2 = (f32[1,1]{1,0:T(1,128)}, f32[1,1]{1,0:T(1,128)}, f32[1,1]{1,0:T(1,128)}, f32[1,1]{1,0:T(1,128)}, f32[1,1]{1,0:T(1,128)}) all-reduce(f32[1,1]{1,0:T(1,128)} %bitcast.57, f32[1,1]{1,0:T(1,128)} %bitcast.54, f32[1,1]{1,0:T(1,128)} %bitcast.58, f32[1,1]{1,0:T(1,128)} %bitcast.59, ...), channel_id=1, replica_groups=mesh['grid'=8,'band'=4] {'grid','band'}, use_global_device_ids=true, to_apply=%region_16.17 | all-reduce | flops 5 | bytes 40 | tf_op jit(solution)/shard_map/psum | solution.py:85
  367.6 14.6 %fusion.66 = f32[4,32,32,64]{3,2,1,0:T(8,128)S(1)} fusion(f32[64,4,32,32]{3,2,1,0:T(8,128)} %reshape.310), kind=kOutput, calls=%fused_computation.50 | convolution fusion | flops 100678656 | bytes 2097152 | tf_op jit(solution)/shard_map/arpyz,wz->pywar/dot_general | solution.py:59
  390.4 19.2 %all_to_all.134 = f32[8,1,32768]{2,1,0:T(1,128)} all-to-all(f32[8,1,32768]{2,1,0:T(1,128)S(1)} %reshape.329), channel_id=1, replica_groups=mesh['grid'=8,'band'=4] {'grid'}, dimensions={0} | all-to-all | bytes 2097152 | tf_op jit(solution)/shard_map/all_to_all | solution.py:65
  409.6 4.4 reduce.25
  429.0 4.6 all-to-all-start.5
  434.3 14.8 %all-to-all-done.5 = f32[8,1,32768]{2,1,0:T(1,128)} async-done(((f32[8,1,32768]{2,1,0:T(1,128)}), f32[8,1,32768]{2,1,0:T(1,128)}, u32[]{:S(2)}, u32[]{:S(2)}) %all-to-all-start.5) | async-done | bytes 1048608 | tf_op jit(solution)/shard_map/all_to_all | solution.py:80
  449.1 4.4 reduce.26
  459.4 4.4 multiply_bitcast_fusion.1
  463.7 5.6 copy.117
  469.3 4.4 div.237
  480.2 42.5 %all-reduce.1 = (f32[1,1]{1,0:T(1,128)}, f32[1,1]{1,0:T(1,128)}, f32[1,1]{1,0:T(1,128)}, f32[1,1]{1,0:T(1,128)}, f32[1,1]{1,0:T(1,128)}) all-reduce(f32[1,1]{1,0:T(1,128)} %bitcast.83, f32[1,1]{1,0:T(1,128)} %bitcast.80, f32[1,1]{1,0:T(1,128)} %bitcast.84, f32[1,1]{1,0:T(1,128)} %bitcast.85, ...), channel_id=1, replica_groups=mesh['grid'=8,'band'=4] {'grid','band'}, use_global_device_ids=true, to_apply=%region_26.27 | all-reduce | flops 5 | bytes 40 | tf_op jit(solution)/shard_map/psum | solution.py:85
  532.2 14.6 %fusion.69 = f32[4,32,32,64]{3,2,1,0:T(8,128)S(1)} fusion(f32[64,4,32,32]{3,2,1,0:T(8,128)} %reshape.315), kind=kOutput, calls=%fused_computation.51 | convolution fusion | flops 100678656 | bytes 2097152 | tf_op jit(solution)/shard_map/arpyz,wz->pywar/dot_general | solution.py:59
  555.0 19.3 %all_to_all.135 = f32[8,1,32768]{2,1,0:T(1,128)} all-to-all(f32[8,1,32768]{2,1,0:T(1,128)S(1)} %reshape.333), channel_id=1, replica_groups=mesh['grid'=8,'band'=4] {'grid'}, dimensions={0} | all-to-all | bytes 2097152 | tf_op jit(solution)/shard_map/all_to_all | solution.py:65
  593.7 4.5 all-to-all-start.7
  598.8 14.8 %all-to-all-done.7 = f32[8,1,32768]{2,1,0:T(1,128)} async-done(((f32[8,1,32768]{2,1,0:T(1,128)}), f32[8,1,32768]{2,1,0:T(1,128)}, u32[]{:S(2)}, u32[]{:S(2)}) %all-to-all-start.7) | async-done | bytes 1048608 | tf_op jit(solution)/shard_map/all_to_all | solution.py:80
  628.2 5.6 copy.127
  633.8 4.4 div.254
  644.8 41.3 %all-reduce = (f32[1,1]{1,0:T(1,128)}, f32[1,1]{1,0:T(1,128)}, f32[1,1]{1,0:T(1,128)}, f32[1,1]{1,0:T(1,128)}, f32[1,1]{1,0:T(1,128)}) all-reduce(f32[1,1]{1,0:T(1,128)} %bitcast.106, f32[1,1]{1,0:T(1,128)} %bitcast.111, f32[1,1]{1,0:T(1,128)} %bitcast.112, ...), channel_id=1, replica_groups=mesh['grid'=8,'band'=4] {'grid','band'}, use_global_device_ids=true, to_apply=%region_34.35 | all-reduce | flops 5 | bytes 40 | tf_op jit(solution)/shard_map/psum | solution.py:85
  (90 shorter events, 183.1 us)
Async XLA Ops:
  69.6 6.2 copy-start.5
  69.6 8.8 %copy-start.4 = (f32[32,32,32]{2,1,0:T(8,128)S(1)}, f32[32,32,32]{2,1,0:T(8,128)}, u32[]{:S(2)}) copy-start(f32[32,32,32]{2,1,0:T(8,128)} %param.7) | copy-start | bytes 393220
  71.8 19.3 %all-to-all-start = ((f32[8,1,32768]{2,1,0:T(1,128)}), f32[8,1,32768]{2,1,0:T(1,128)S(1)}, u32[]{:S(2)}, u32[]{:S(2)}) async-start(f32[8,1,32768]{2,1,0:T(1,128)} %reshape.321), calls=%async_computation | async-start | bytes 2097152 | tf_op jit(solution)/shard_map/all_to_all | solution.py:65
  135.5 3.7 copy-start
  135.5 3.7 copy-start.1
  263.0 20.0 %all-to-all-start.3 = ((f32[8,1,32768]{2,1,0:T(1,128)}), f32[8,1,32768]{2,1,0:T(1,128)}, u32[]{:S(2)}, u32[]{:S(2)}) async-start(f32[8,1,32768]{2,1,0:T(1,128)} %reshape.327), calls=%async_computation.3 | async-start | bytes 2097152 | tf_op jit(solution)/shard_map/all_to_all | solution.py:80
  429.0 20.0 %all-to-all-start.5 = ((f32[8,1,32768]{2,1,0:T(1,128)}), f32[8,1,32768]{2,1,0:T(1,128)}, u32[]{:S(2)}, u32[]{:S(2)}) async-start(f32[8,1,32768]{2,1,0:T(1,128)} %reshape.331), calls=%async_computation.5 | async-start | bytes 2097152 | tf_op jit(solution)/shard_map/all_to_all | solution.py:80
  469.3 4.4 copy-start.2
  593.7 19.9 %all-to-all-start.7 = ((f32[8,1,32768]{2,1,0:T(1,128)}), f32[8,1,32768]{2,1,0:T(1,128)}, u32[]{:S(2)}, u32[]{:S(2)}) async-start(f32[8,1,32768]{2,1,0:T(1,128)} %reshape.335), calls=%async_computation.7 | async-start | bytes 2097152 | tf_op jit(solution)/shard_map/all_to_all | solution.py:80
  633.8 4.4 copy-start.3
where the time goes:
time: 709 us; the launch traced here: 698 us
  blocking collectives  287 us (40%)
  local copies, waits for them, and re-layouts  118 us (17%)
  matrix products  115 us (16%)
  other arithmetic  62.4 us (9%)
  waiting for transfers between devices  56.4 us (8%)
  between operations  40.5 us (6%)
  starting transfers between devices  17.7 us (2%)
    psum x4, blocking collectives, body(): lax.psum((moment(lanczos, applied), moment(applied, applied), moment(lanc...  168 us
    dot_general x4, matrix products, body(): jnp.einsum('arpyz,wz->pywar', spread_fields, cas_grid, precision=precise_...  58.4 us
    all_to_all x3, blocking collectives, body(): lax.all_to_all(spread_over_y.reshape(plane_count, grid_size, grid_size, f...  58.3 us
    all_to_all x3, waiting for transfers between devices, body(): lax.all_to_all(weighted, 'grid', split_axis=0, concat_axis=1, tiled=True)  44.3 us
    psum x1, blocking collectives, body(): start_sum = lax.psum(moment(start, start), ('grid', 'band'))  42.7 us
    unnamed x28, local copies, waits for them, and re-layouts  39.2 us
    div x8, local copies, waits for them, and re-layouts, body(): over_y.reshape(start.shape) / volume  38.1 us
    all_to_all x1, blocking collectives, body(): lax.all_to_all(weighted, 'grid', split_axis=0, concat_axis=1, tiled=True)  18.2 us
  transfers between devices with their start and end apart: 4, of which 4 were waited for; matrix products, arithmetic and copies ran while one was open for 0% of the time, Pallas kernels for 0%

commit v1 on v0

--- a/solution.py
+++ b/solution.py
@@ -6,6 +6,18 @@
 
 ITERS = 4
 precise_mode = lax.Precision.HIGHEST
+
+
+def cut_along(x, dim, size):
+    lengths = x.shape
+    blocks = x.reshape(*lengths[:dim], size, lengths[dim] // size, *lengths[dim + 1 :])
+    return jnp.moveaxis(blocks, dim, 0)
+
+
+def in_order(pieces, dim):
+    pieces = jnp.moveaxis(pieces, 0, dim)
+    dims = pieces.shape
+    return pieces.reshape(*dims[:dim], dims[dim] * dims[dim + 1], *dims[dim + 2 :])
 
 
 def cas_table(grid_size):
@@ -77,7 +89,14 @@
         scaled = split_view * slab_table[..., None]
         back_x = jnp.einsum("tvwar,xt->xvwar", scaled, cas_grid, precision=precise_mode)
         weighted = back_x.reshape(field_shape)
-        direct_returned = lax.all_to_all(weighted, "grid", split_axis=0, concat_axis=1, tiled=True)
+        size, index = (lax.axis_size("grid"), lax.axis_index("grid"))
+        tiles = cut_along(weighted, 0, size)
+        outs = [tiles[index]]
+        for step in range(1, size):
+            sent = tiles[index ^ step]
+            outs.append(lax.ppermute(sent, "grid", [(i, i ^ step) for i in range(size)]))
+        tiles = jnp.stack(outs)[index ^ jnp.arange(size)]
+        direct_returned = in_order(tiles, 1)
         fields = direct_returned.reshape(plane_count, grid_size, grid_size, atom_count, chain_count)
         over_z = jnp.einsum("pvwar,zw->pvzar", fields, cas_grid, precision=precise_mode)
         over_y = jnp.einsum("pvzar,yv->arpyz", over_z, cas_grid, precision=precise_mode)

time: 709 us -> 756 us (1.066)
  waiting for transfers between devices: 56.4 us -> 99.7 us
  local copies, waits for them, and re-layouts: 118 us -> 152 us
  blocking collectives: 287 us -> 269 us
  other arithmetic: 62.4 us -> 45.2 us
    ppermute x0 -> x28, waiting for transfers between devices: none -> 87.8 us  [body(): lax.ppermute(sent, 'grid', [(i, i ^ step) for i in range(size)])]
    all_to_all x3 -> x0, waiting for transfers between devices: 44.3 us -> none  [body(): lax.all_to_all(weighted, 'grid', split_axis=0, concat_axis=1, tiled=True)]
    another operation x4 -> x12, local copies, waits for them, and re-layouts: 10.8 us -> 48 us  [the longest x8 37.2 us: body(): tiles = jnp.stack(outs)[index ^ jnp.arange(size)]]
    all_to_all x1 -> x0, blocking collectives: 18.2 us -> none  [body(): lax.all_to_all(weighted, 'grid', split_axis=0, concat_axis=1, tiled=True)]
    all_to_all x4 -> x0, other arithmetic: 17.2 us -> none  [body(): lax.all_to_all(weighted, 'grid', split_axis=0, concat_axis=1, tiled=True)]
    ppermute x0 -> x28, starting transfers between devices: none -> 16.8 us  [body(): lax.ppermute(sent, 'grid', [(i, i ^ step) for i in range(size)])]
    unnamed x28 -> x66, local copies, waits for them, and re-layouts: 39.2 us -> 22.7 us
    all_to_all x3 -> x0, starting transfers between devices: 13.8 us -> none  [body(): lax.all_to_all(weighted, 'grid', split_axis=0, concat_axis=1, tiled=True)]
  transfers between devices with their start and end apart: 4 -> 29, of which waited for: 4 -> 13; matrix products, arithmetic and copies ran while one was open for 0% -> 0% of each run, Pallas kernels for 0% -> 0%
where the time goes in v1:
time: 756 us; the launch traced here: 743 us
  blocking collectives  269 us (36%)
  local copies, waits for them, and re-layouts  152 us (20%)
  matrix products  115 us (15%)
  waiting for transfers between devices  99.7 us (13%)
  other arithmetic  45.2 us (6%)
  between operations  41.2 us (5%)
  starting transfers between devices  20.7 us (3%)
    psum x4, blocking collectives, body(): lax.psum((moment(lanczos, applied), moment(applied, applied), moment(lanc...  168 us
    ppermute x28, waiting for transfers between devices, body(): lax.ppermute(sent, 'grid', [(i, i ^ step) for i in range(size)])  87.8 us
    dot_general x4, matrix products, body(): jnp.einsum('arpyz,wz->pywar', spread_fields, cas_grid, precision=precise_...  58.4 us
    all_to_all x3, blocking collectives, body(): lax.all_to_all(spread_over_y.reshape(plane_count, grid_size, grid_size, f...  58.3 us
    psum x1, blocking collectives, body(): start_sum = lax.psum(moment(start, start), ('grid', 'band'))  42.7 us
    div x8, local copies, waits for them, and re-layouts, body(): over_y.reshape(start.shape) / volume  38.1 us
    another operation x8, local copies, waits for them, and re-layouts, body(): tiles = jnp.stack(outs)[index ^ jnp.arange(size)]  37.2 us
    unnamed x66, local copies, waits for them, and re-layouts  22.7 us
  transfers between devices with their start and end apart: 29, of which 13 were waited for; matrix products, arithmetic and copies ran while one was open for 0% of the time, Pallas kernels for 0%

profile of v1, /device:TPU:0, one launch (start us, length us, event | category | flops | bytes accessed | tf_op | source)
XLA Modules:
  0.0 743.3 jit_solution(16079092427340174976)
XLA Ops:
  3.4 42.7 %psum.163 = f32[1,1]{1,0:T(1,128)} all-reduce(f32[1,1]{1,0:T(1,128)} %bitcast.1), channel_id=1, replica_groups=mesh['grid'=8,'band'=4] {'grid','band'}, use_global_device_ids=true, to_apply=%region_1.2 | all-reduce | flops 1 | bytes 8 | tf_op jit(solution)/shard_map/psum | solution.py:63
  50.8 14.6 %fusion.64 = f32[4,32,32,64]{3,2,1,0:T(8,128)S(1)} fusion(f32[64,4,32,32]{3,2,1,0:T(8,128)} %reshape.365), kind=kOutput, calls=%fused_computation.56 | convolution fusion | flops 100678656 | bytes 2097152 | tf_op jit(solution)/shard_map/arpyz,wz->pywar/dot_general | solution.py:71
  79.0 11.9 %all-to-all-done = f32[8,1,32768]{2,1,0:T(1,128)S(1)} async-done(((f32[8,1,32768]{2,1,0:T(1,128)}), f32[8,1,32768]{2,1,0:T(1,128)S(1)}, u32[]{:S(2)}, u32[]{:S(2)}) %all-to-all-start) | async-done | bytes 1048608 | tf_op jit(solution)/shard_map/all_to_all | solution.py:77
  107.3 5.1 collective-permute-done.1
  116.9 12.9 %collective-permute-done.4 = f32[4,4,32,64]{3,2,1,0:T(8,128)S(1)} collective-permute-done((f32[4,4,32,64]{3,2,1,0:T(8,128)S(1)}, f32[4,4,32,64]{3,2,1,0:T(8,128)S(1)}, u32[]{:S(2)}, u32[]{:S(2)}) %collective-permute-start.4) | collective-permute-done | bytes 131104 | tf_op jit(solution)/shard_map/ppermute | solution.py:97
  130.7 5.2 stack.134
  145.2 4.5 copy.97
  158.7 43.0 %all-reduce.3 = (f32[1,1]{1,0:T(1,128)}, f32[1,1]{1,0:T(1,128)}, f32[1,1]{1,0:T(1,128)}, f32[1,1]{1,0:T(1,128)}, f32[1,1]{1,0:T(1,128)}, /*index=5*/f32[1,1]{1,0:T(1,128)}) all-reduce(f32[1,1]{1,0:T(1,128)} %bitcast.48, f32[1,1]{1,0:T(1,128)} %bitcast.45, f32[1,1]{1,0:T(1,128)} %bitcast.49, ...), channel_id=1, replica_groups=mesh['grid'=8,'band'=4] {'grid','band'}, use_global_device_ids=true, to_apply=%region_5.6 | all-reduce | flops 6 | bytes 48 | tf_op jit(solution)/shard_map/psum | solution.py:104
  212.3 14.6 %fusion.67 = f32[4,32,32,64]{3,2,1,0:T(8,128)S(1)} fusion(f32[64,4,32,32]{3,2,1,0:T(8,128)} %reshape.370), kind=kOutput, calls=%fused_computation.57 | convolution fusion | flops 100678656 | bytes 2097152 | tf_op jit(solution)/shard_map/arpyz,wz->pywar/dot_general | solution.py:71
  235.9 19.8 %all_to_all.72 = f32[8,1,32768]{2,1,0:T(1,128)} all-to-all(f32[8,1,32768]{2,1,0:T(1,128)} %reshape.425), channel_id=1, replica_groups=mesh['grid'=8,'band'=4] {'grid'}, dimensions={0} | all-to-all | bytes 2097152 | tf_op jit(solution)/shard_map/all_to_all | solution.py:77
  255.7 5.3 reduce.22
  277.9 5.1 collective-permute-done.8
  287.6 12.9 %collective-permute-done.11 = f32[4,4,32,64]{3,2,1,0:T(8,128)S(1)} collective-permute-done((f32[4,4,32,64]{3,2,1,0:T(8,128)S(1)}, f32[4,4,32,64]{3,2,1,0:T(8,128)S(1)}, u32[]{:S(2)}, u32[]{:S(2)}) %collective-permute-start.11) | collective-permute-done | bytes 131104 | tf_op jit(solution)/shard_map/ppermute | solution.py:97
  301.3 6.9 stack.143
  323.2 5.6 copy.107
  339.6 41.5 %all-reduce.2 = (f32[1,1]{1,0:T(1,128)}, f32[1,1]{1,0:T(1,128)}, f32[1,1]{1,0:T(1,128)}, f32[1,1]{1,0:T(1,128)}, f32[1,1]{1,0:T(1,128)}) all-reduce(f32[1,1]{1,0:T(1,128)} %bitcast.89, f32[1,1]{1,0:T(1,128)} %bitcast.86, f32[1,1]{1,0:T(1,128)} %bitcast.90, f32[1,1]{1,0:T(1,128)} %bitcast.91, ...), channel_id=1, replica_groups=mesh['grid'=8,'band'=4] {'grid','band'}, use_global_device_ids=true, to_apply=%region_16.17 | all-reduce | flops 5 | bytes 40 | tf_op jit(solution)/shard_map/psum | solution.py:104
  390.8 14.6 %fusion.70 = f32[4,32,32,64]{3,2,1,0:T(8,128)S(1)} fusion(f32[64,4,32,32]{3,2,1,0:T(8,128)} %reshape.375), kind=kOutput, calls=%fused_computation.58 | convolution fusion | flops 100678656 | bytes 2097152 | tf_op jit(solution)/shard_map/arpyz,wz->pywar/dot_general | solution.py:71
  413.6 19.2 %all_to_all.73 = f32[8,1,32768]{2,1,0:T(1,128)} all-to-all(f32[8,1,32768]{2,1,0:T(1,128)S(1)} %reshape.427), channel_id=1, replica_groups=mesh['grid'=8,'band'=4] {'grid'}, dimensions={0} | all-to-all | bytes 2097152 | tf_op jit(solution)/shard_map/all_to_all | solution.py:77
  452.9 5.1 collective-permute-done.15
  462.5 12.9 %collective-permute-done.18 = f32[4,4,32,64]{3,2,1,0:T(8,128)S(1)} collective-permute-done((f32[4,4,32,64]{3,2,1,0:T(8,128)S(1)}, f32[4,4,32,64]{3,2,1,0:T(8,128)S(1)}, u32[]{:S(2)}, u32[]{:S(2)}) %collective-permute-start.18) | collective-permute-done | bytes 131104 | tf_op jit(solution)/shard_map/ppermute | solution.py:97
  476.3 6.8 stack.152
  498.0 5.6 copy.117
  503.7 4.4 div.237
  514.5 42.4 %all-reduce.1 = (f32[1,1]{1,0:T(1,128)}, f32[1,1]{1,0:T(1,128)}, f32[1,1]{1,0:T(1,128)}, f32[1,1]{1,0:T(1,128)}, f32[1,1]{1,0:T(1,128)}) all-reduce(f32[1,1]{1,0:T(1,128)} %bitcast.129, f32[1,1]{1,0:T(1,128)} %bitcast.126, f32[1,1]{1,0:T(1,128)} %bitcast.130, ...), channel_id=1, replica_groups=mesh['grid'=8,'band'=4] {'grid','band'}, use_global_device_ids=true, to_apply=%region_26.27 | all-reduce | flops 5 | bytes 40 | tf_op jit(solution)/shard_map/psum | solution.py:104
  566.4 14.6 %fusion.73 = f32[4,32,32,64]{3,2,1,0:T(8,128)S(1)} fusion(f32[64,4,32,32]{3,2,1,0:T(8,128)} %reshape.380), kind=kOutput, calls=%fused_computation.59 | convolution fusion | flops 100678656 | bytes 2097152 | tf_op jit(solution)/shard_map/arpyz,wz->pywar/dot_general | solution.py:71
  589.2 19.3 %all_to_all.74 = f32[8,1,32768]{2,1,0:T(1,128)} all-to-all(f32[8,1,32768]{2,1,0:T(1,128)S(1)} %reshape.429), channel_id=1, replica_groups=mesh['grid'=8,'band'=4] {'grid'}, dimensions={0} | all-to-all | bytes 2097152 | tf_op jit(solution)/shard_map/all_to_all | solution.py:77
  628.5 5.1 collective-permute-done.22
  638.2 12.9 %collective-permute-done.25 = f32[4,4,32,64]{3,2,1,0:T(8,128)S(1)} collective-permute-done((f32[4,4,32,64]{3,2,1,0:T(8,128)S(1)}, f32[4,4,32,64]{3,2,1,0:T(8,128)S(1)}, u32[]{:S(2)}, u32[]{:S(2)}) %collective-permute-start.25) | collective-permute-done | bytes 131104 | tf_op jit(solution)/shard_map/ppermute | solution.py:97
  652.0 6.7 stack.161
  673.7 5.6 copy.127
  679.3 4.4 div.254
  690.2 41.2 %all-reduce = (f32[1,1]{1,0:T(1,128)}, f32[1,1]{1,0:T(1,128)}, f32[1,1]{1,0:T(1,128)}, f32[1,1]{1,0:T(1,128)}, f32[1,1]{1,0:T(1,128)}) all-reduce(f32[1,1]{1,0:T(1,128)} %bitcast.166, f32[1,1]{1,0:T(1,128)} %bitcast.171, f32[1,1]{1,0:T(1,128)} %bitcast.172, ...), channel_id=1, replica_groups=mesh['grid'=8,'band'=4] {'grid','band'}, use_global_device_ids=true, to_apply=%region_34.35 | all-reduce | flops 5 | bytes 40 | tf_op jit(solution)/shard_map/psum | solution.py:104
  (188 shorter events, 229.7 us)
Async XLA Ops:
  71.8 19.1 %all-to-all-start = ((f32[8,1,32768]{2,1,0:T(1,128)}), f32[8,1,32768]{2,1,0:T(1,128)S(1)}, u32[]{:S(2)}, u32[]{:S(2)}) async-start(f32[8,1,32768]{2,1,0:T(1,128)} %reshape.423), calls=%async_computation | async-start | bytes 2097152 | tf_op jit(solution)/shard_map/all_to_all | solution.py:77
  103.1 3.6 collective-permute-start
  103.1 9.2 %collective-permute-start.1 = (f32[4,4,32,64]{3,2,1,0:T(8,128)S(1)}, f32[4,4,32,64]{3,2,1,0:T(8,128)S(1)}, u32[]{:S(2)}, u32[]{:S(2)}) collective-permute-start(f32[4,4,32,64]{3,2,1,0:T(8,128)S(1)} %bitcast.416), channel_id=1, source_target_pairs={{0,8},{4,12},{8,0},{12,4},{16,24},{20,28},{24,16},{28,20},{1,9},{5... | collective-permute-start | bytes 393224 | tf_op jit(solution)/shard_map/ppermute | solution.py:97
  103.7 13.2 %collective-permute-start.2 = (f32[4,4,32,64]{3,2,1,0:T(8,128)S(1)}, f32[4,4,32,64]{3,2,1,0:T(8,128)S(1)}, u32[]{:S(2)}, u32[]{:S(2)}) collective-permute-start(f32[4,4,32,64]{3,2,1,0:T(8,128)S(1)} %bitcast.408), channel_id=1, source_target_pairs={{0,12},{4,8},{8,4},{12,0},{16,28},{20,24},{24,20},{28,16},{1,13},{... | collective-permute-start | bytes 393224 | tf_op jit(solution)/shard_map/ppermute | solution.py:97
  105.0 11.9 %collective-permute-start.3 = (f32[4,4,32,64]{3,2,1,0:T(8,128)S(1)}, f32[4,4,32,64]{3,2,1,0:T(8,128)S(1)}, u32[]{:S(2)}, u32[]{:S(2)}) collective-permute-start(f32[4,4,32,64]{3,2,1,0:T(8,128)S(1)} %bitcast.401), channel_id=1, source_target_pairs={{0,16},{4,20},{8,24},{12,28},{16,0},{20,4},{24,8},{28,12},{1,17},{... | collective-permute-start | bytes 393224 | tf_op jit(solution)/shard_map/ppermute | solution.py:97
  105.6 24.2 %collective-permute-start.4 = (f32[4,4,32,64]{3,2,1,0:T(8,128)S(1)}, f32[4,4,32,64]{3,2,1,0:T(8,128)S(1)}, u32[]{:S(2)}, u32[]{:S(2)}) collective-permute-start(f32[4,4,32,64]{3,2,1,0:T(8,128)S(1)} %bitcast.394), channel_id=1, source_target_pairs={{0,20},{4,16},{8,28},{12,24},{16,4},{20,0},{24,12},{28,8},{1,21},{... | collective-permute-start | bytes 393224 | tf_op jit(solution)/shard_map/ppermute | solution.py:97
  106.7 23.1 %collective-permute-start.5 = (f32[4,4,32,64]{3,2,1,0:T(8,128)S(1)}, f32[4,4,32,64]{3,2,1,0:T(8,128)S(1)}, u32[]{:S(2)}, u32[]{:S(2)}) collective-permute-start(f32[4,4,32,64]{3,2,1,0:T(8,128)S(1)} %bitcast.386), channel_id=1, source_target_pairs={{0,24},{4,28},{8,16},{12,20},{16,8},{20,12},{24,0},{28,4},{1,25},{... | collective-permute-start | bytes 393224 | tf_op jit(solution)/shard_map/ppermute | solution.py:97
  112.4 17.4 %collective-permute-start.6 = (f32[4,4,32,64]{3,2,1,0:T(8,128)S(1)}, f32[4,4,32,64]{3,2,1,0:T(8,128)S(1)}, u32[]{:S(2)}, u32[]{:S(2)}) collective-permute-start(f32[4,4,32,64]{3,2,1,0:T(8,128)S(1)} %bitcast.378), channel_id=1, source_target_pairs={{0,28},{4,24},{8,20},{12,16},{16,12},{20,8},{24,4},{28,0},{1,29},{... | collective-permute-start | bytes 393224 | tf_op jit(solution)/shard_map/ppermute | solution.py:97
  273.7 3.6 collective-permute-start.7
  273.8 9.2 %collective-permute-start.8 = (f32[4,4,32,64]{3,2,1,0:T(8,128)S(1)}, f32[4,4,32,64]{3,2,1,0:T(8,128)S(1)}, u32[]{:S(2)}, u32[]{:S(2)}) collective-permute-start(f32[4,4,32,64]{3,2,1,0:T(8,128)S(1)} %bitcast.417), channel_id=1, source_target_pairs={{0,8},{4,12},{8,0},{12,4},{16,24},{20,28},{24,16},{28,20},{1,9},{5... | collective-permute-start | bytes 393224 | tf_op jit(solution)/shard_map/ppermute | solution.py:97
  274.4 13.2 %collective-permute-start.9 = (f32[4,4,32,64]{3,2,1,0:T(8,128)S(1)}, f32[4,4,32,64]{3,2,1,0:T(8,128)S(1)}, u32[]{:S(2)}, u32[]{:S(2)}) collective-permute-start(f32[4,4,32,64]{3,2,1,0:T(8,128)S(1)} %bitcast.403), channel_id=1, source_target_pairs={{0,12},{4,8},{8,4},{12,0},{16,28},{20,24},{24,20},{28,16},{1,13},{... | collective-permute-start | bytes 393224 | tf_op jit(solution)/shard_map/ppermute | solution.py:97
  275.6 11.9 %collective-permute-start.10 = (f32[4,4,32,64]{3,2,1,0:T(8,128)S(1)}, f32[4,4,32,64]{3,2,1,0:T(8,128)S(1)}, u32[]{:S(2)}, u32[]{:S(2)}) collective-permute-start(f32[4,4,32,64]{3,2,1,0:T(8,128)S(1)} %bitcast.396), channel_id=1, source_target_pairs={{0,16},{4,20},{8,24},{12,28},{16,0},{20,4},{24,8},{28,12},{1,17},{... | collective-permute-start | bytes 393224 | tf_op jit(solution)/shard_map/ppermute | solution.py:97
  276.2 24.3 %collective-permute-start.11 = (f32[4,4,32,64]{3,2,1,0:T(8,128)S(1)}, f32[4,4,32,64]{3,2,1,0:T(8,128)S(1)}, u32[]{:S(2)}, u32[]{:S(2)}) collective-permute-start(f32[4,4,32,64]{3,2,1,0:T(8,128)S(1)} %bitcast.389), channel_id=1, source_target_pairs={{0,20},{4,16},{8,28},{12,24},{16,4},{20,0},{24,12},{28,8},{1,21},{... | collective-permute-start | bytes 393224 | tf_op jit(solution)/shard_map/ppermute | solution.py:97
  277.4 23.1 %copy-start.5 = (f32[4,4,32,64]{3,2,1,0:T(8,128)}, f32[4,4,32,64]{3,2,1,0:T(8,128)S(1)}, u32[]{:S(2)}) copy-start(f32[4,4,32,64]{3,2,1,0:T(8,128)S(1)} %collective-permute-done.7) | copy-start | bytes 393220
  277.4 23.1 %collective-permute-start.12 = (f32[4,4,32,64]{3,2,1,0:T(8,128)S(1)}, f32[4,4,32,64]{3,2,1,0:T(8,128)S(1)}, u32[]{:S(2)}, u32[]{:S(2)}) collective-permute-start(f32[4,4,32,64]{3,2,1,0:T(8,128)S(1)} %bitcast.381), channel_id=1, source_target_pairs={{0,24},{4,28},{8,16},{12,20},{16,8},{20,12},{24,0},{28,4},{1,25},{... | collective-permute-start | bytes 393224 | tf_op jit(solution)/shard_map/ppermute | solution.py:97
  283.0 17.4 %copy-start.6 = (f32[4,4,32,64]{3,2,1,0:T(8,128)}, f32[4,4,32,64]{3,2,1,0:T(8,128)S(1)}, u32[]{:S(2)}) copy-start(f32[4,4,32,64]{3,2,1,0:T(8,128)S(1)} %collective-permute-done.8) | copy-start | bytes 393220
  283.0 17.4 %collective-permute-start.13 = (f32[4,4,32,64]{3,2,1,0:T(8,128)S(1)}, f32[4,4,32,64]{3,2,1,0:T(8,128)S(1)}, u32[]{:S(2)}, u32[]{:S(2)}) collective-permute-start(f32[4,4,32,64]{3,2,1,0:T(8,128)S(1)} %bitcast.373), channel_id=1, source_target_pairs={{0,28},{4,24},{8,20},{12,16},{16,12},{20,8},{24,4},{28,0},{1,29},{... | collective-permute-start | bytes 393224 | tf_op jit(solution)/shard_map/ppermute | solution.py:97
  448.6 3.6 collective-permute-start.14
  448.7 9.2 %collective-permute-start.15 = (f32[4,4,32,64]{3,2,1,0:T(8,128)S(1)}, f32[4,4,32,64]{3,2,1,0:T(8,128)S(1)}, u32[]{:S(2)}, u32[]{:S(2)}) collective-permute-start(f32[4,4,32,64]{3,2,1,0:T(8,128)S(1)} %bitcast.418), channel_id=1, source_target_pairs={{0,8},{4,12},{8,0},{12,4},{16,24},{20,28},{24,16},{28,20},{1,9},{5... | collective-permute-start | bytes 393224 | tf_op jit(solution)/shard_map/ppermute | solution.py:97
  449.3 13.2 %collective-permute-start.16 = (f32[4,4,32,64]{3,2,1,0:T(8,128)S(1)}, f32[4,4,32,64]{3,2,1,0:T(8,128)S(1)}, u32[]{:S(2)}, u32[]{:S(2)}) collective-permute-start(f32[4,4,32,64]{3,2,1,0:T(8,128)S(1)} %bitcast.405), channel_id=1, source_target_pairs={{0,12},{4,8},{8,4},{12,0},{16,28},{20,24},{24,20},{28,16},{1,13},{... | collective-permute-start | bytes 393224 | tf_op jit(solution)/shard_map/ppermute | solution.py:97
  450.6 11.9 %collective-permute-start.17 = (f32[4,4,32,64]{3,2,1,0:T(8,128)S(1)}, f32[4,4,32,64]{3,2,1,0:T(8,128)S(1)}, u32[]{:S(2)}, u32[]{:S(2)}) collective-permute-start(f32[4,4,32,64]{3,2,1,0:T(8,128)S(1)} %bitcast.398), channel_id=1, source_target_pairs={{0,16},{4,20},{8,24},{12,28},{16,0},{20,4},{24,8},{28,12},{1,17},{... | collective-permute-start | bytes 393224 | tf_op jit(solution)/shard_map/ppermute | solution.py:97
  451.1 24.2 %collective-permute-start.18 = (f32[4,4,32,64]{3,2,1,0:T(8,128)S(1)}, f32[4,4,32,64]{3,2,1,0:T(8,128)S(1)}, u32[]{:S(2)}, u32[]{:S(2)}) collective-permute-start(f32[4,4,32,64]{3,2,1,0:T(8,128)S(1)} %bitcast.391), channel_id=1, source_target_pairs={{0,20},{4,16},{8,28},{12,24},{16,4},{20,0},{24,12},{28,8},{1,21},{... | collective-permute-start | bytes 393224 | tf_op jit(solution)/shard_map/ppermute | solution.py:97
  452.3 23.1 %collective-permute-start.19 = (f32[4,4,32,64]{3,2,1,0:T(8,128)S(1)}, f32[4,4,32,64]{3,2,1,0:T(8,128)S(1)}, u32[]{:S(2)}, u32[]{:S(2)}) collective-permute-start(f32[4,4,32,64]{3,2,1,0:T(8,128)S(1)} %bitcast.383), channel_id=1, source_target_pairs={{0,24},{4,28},{8,16},{12,20},{16,8},{20,12},{24,0},{28,4},{1,25},{... | collective-permute-start | bytes 393224 | tf_op jit(solution)/shard_map/ppermute | solution.py:97
  458.0 17.4 %collective-permute-start.20 = (f32[4,4,32,64]{3,2,1,0:T(8,128)S(1)}, f32[4,4,32,64]{3,2,1,0:T(8,128)S(1)}, u32[]{:S(2)}, u32[]{:S(2)}) collective-permute-start(f32[4,4,32,64]{3,2,1,0:T(8,128)S(1)} %bitcast.375), channel_id=1, source_target_pairs={{0,28},{4,24},{8,20},{12,16},{16,12},{20,8},{24,4},{28,0},{1,29},{... | collective-permute-start | bytes 393224 | tf_op jit(solution)/shard_map/ppermute | solution.py:97
  624.3 3.6 collective-permute-start.21
  624.4 9.2 %collective-permute-start.22 = (f32[4,4,32,64]{3,2,1,0:T(8,128)S(1)}, f32[4,4,32,64]{3,2,1,0:T(8,128)S(1)}, u32[]{:S(2)}, u32[]{:S(2)}) collective-permute-start(f32[4,4,32,64]{3,2,1,0:T(8,128)S(1)} %bitcast.410), channel_id=1, source_target_pairs={{0,8},{4,12},{8,0},{12,4},{16,24},{20,28},{24,16},{28,20},{1,9},{5... | collective-permute-start | bytes 393224 | tf_op jit(solution)/shard_map/ppermute | solution.py:97
  625.0 13.2 %collective-permute-start.23 = (f32[4,4,32,64]{3,2,1,0:T(8,128)S(1)}, f32[4,4,32,64]{3,2,1,0:T(8,128)S(1)}, u32[]{:S(2)}, u32[]{:S(2)}) collective-permute-start(f32[4,4,32,64]{3,2,1,0:T(8,128)S(1)} %bitcast.388), channel_id=1, source_target_pairs={{0,12},{4,8},{8,4},{12,0},{16,28},{20,24},{24,20},{28,16},{1,13},{... | collective-permute-start | bytes 393224 | tf_op jit(solution)/shard_map/ppermute | solution.py:97
  626.3 11.9 %collective-permute-start.24 = (f32[4,4,32,64]{3,2,1,0:T(8,128)S(1)}, f32[4,4,32,64]{3,2,1,0:T(8,128)S(1)}, u32[]{:S(2)}, u32[]{:S(2)}) collective-permute-start(f32[4,4,32,64]{3,2,1,0:T(8,128)S(1)} %bitcast.380), channel_id=1, source_target_pairs={{0,16},{4,20},{8,24},{12,28},{16,0},{20,4},{24,8},{28,12},{1,17},{... | collective-permute-start | bytes 393224 | tf_op jit(solution)/shard_map/ppermute | solution.py:97
  626.8 24.2 %collective-permute-start.25 = (f32[4,4,32,64]{3,2,1,0:T(8,128)S(1)}, f32[4,4,32,64]{3,2,1,0:T(8,128)S(1)}, u32[]{:S(2)}, u32[]{:S(2)}) collective-permute-start(f32[4,4,32,64]{3,2,1,0:T(8,128)S(1)} %bitcast.372), channel_id=1, source_target_pairs={{0,20},{4,16},{8,28},{12,24},{16,4},{20,0},{24,12},{28,8},{1,21},{... | collective-permute-start | bytes 393224 | tf_op jit(solution)/shard_map/ppermute | solution.py:97
  628.0 23.1 %collective-permute-start.26 = (f32[4,4,32,64]{3,2,1,0:T(8,128)S(1)}, f32[4,4,32,64]{3,2,1,0:T(8,128)S(1)}, u32[]{:S(2)}, u32[]{:S(2)}) collective-permute-start(f32[4,4,32,64]{3,2,1,0:T(8,128)S(1)} %bitcast.371), channel_id=1, source_target_pairs={{0,24},{4,28},{8,16},{12,20},{16,8},{20,12},{24,0},{28,4},{1,25},{... | collective-permute-start | bytes 393224 | tf_op jit(solution)/shard_map/ppermute | solution.py:97
  633.7 17.4 %copy-start.7 = (f32[4,4,32,64]{3,2,1,0:T(8,128)}, f32[4,4,32,64]{3,2,1,0:T(8,128)S(1)}, u32[]{:S(2)}) copy-start(f32[4,4,32,64]{3,2,1,0:T(8,128)S(1)} %collective-permute-done.22) | copy-start | bytes 393220
  633.7 17.4 %collective-permute-start.27 = (f32[4,4,32,64]{3,2,1,0:T(8,128)S(1)}, f32[4,4,32,64]{3,2,1,0:T(8,128)S(1)}, u32[]{:S(2)}, u32[]{:S(2)}) collective-permute-start(f32[4,4,32,64]{3,2,1,0:T(8,128)S(1)} %bitcast.370), channel_id=1, source_target_pairs={{0,28},{4,24},{8,20},{12,16},{16,12},{20,8},{24,4},{28,0},{1,29},{... | collective-permute-start | bytes 393224 | tf_op jit(solution)/shard_map/ppermute | solution.py:97
  (26 other events, 143.8 us)
